TPU v7x, 256 devices: a 8x8x2 block of a 8x8x16 slice. The times are simulated.
256 devices in a mesh: parts: 2 (over z), seq: 128 (over x, y, core).
Axes of the slice: x: 8, y: 8, z: 2, core: 2. Of those that a mesh axis runs over, the one named last changes fastest.
The devices are a block of a 8x8x16 slice.
Arguments:
- token_ids: int32 [4, 4], P(None, 'parts'), parts along dimension 1, may hold values from 0 to 76031
- lengths: int32 [4], P('parts'), parts along dimension 0, may hold values from 24576 to 32768, as said below
- embed_table: bfloat16 [76032, 5120], P('seq'), may hold values from -6 to 6
- attn_gain: bfloat16 [5120], replicated, may hold values from 0.25 to 1.75
- w_qkv: bfloat16 [5120, 7168], P('seq'), may hold values from -0.3125 to 0.3125
- qkv_bias: float32 [7168], replicated, may hold values from -8 to 8
- cache_keys: bfloat16 [4, 32768, 1024], P('parts', 'seq'), parts along dimension 0, may hold values from -300 to 300
- cache_values: bfloat16 [4, 32768, 1024], P('parts', 'seq'), parts along dimension 0, may hold values from -6 to 6
- w_out: bfloat16 [5120, 5120], P(None, 'seq'), may hold values from -0.078125 to 0.078125
- mlp_gain: bfloat16 [5120], replicated, may hold values from 0.25 to 1.75
- w_gate: bfloat16 [5120, 16384], P(None, 'seq'), may hold values from -0.078125 to 0.078125
- w_up: bfloat16 [5120, 16384], P(None, 'seq'), may hold values from -0.078125 to 0.078125
- w_down: bfloat16 [16384, 5120], P('seq'), may hold values from -0.1875 to 0.1875
Outputs:
- attended: bfloat16 [4, 4, 5120], P(None, 'parts'), parts along dimension 1
- layer_out: bfloat16 [4, 4, 5120], P(None, 'parts', 'seq'), parts along dimension 1
There are 2 independent parts, one for each index of `parts`. A program takes and returns all parts, laid end to end along the dimension named above; an argument that names none is the same for every part. Nothing has to cross between parts.
Inputs may be any that keep to these rules, and one draw needn't show every extreme that they name: Cache positions lengths[b] and later are unused; the first prompt fills the whole cache of 32768 positions.
All inputs are finite; a program needn't handle non-finite values.
Results may differ from a plain program's by a relative error of at most 0.017.
The roundings to bfloat16 on the way count: a program that leaves them out, or rounds other values in their place, can miss the bound.
Values may be sent and summed in bfloat16 or wider, within the bound.
No kernel may reach another device: no remote copies, remote signals or barrier semaphores. Data moves between devices by JAX's collectives and lax.ppermute only.
A program may use at most 128 MiB of HBM per device.

v0:
```python
import math
import jax
import jax.numpy as jnp
from jax import lax
from jax.sharding import Mesh
from jax.sharding import PartitionSpec as P

HEADS = 40
KV_HEADS = 8
HEAD_DIM = 128
SEQ = ("seq_0", "seq_1", "seq_2")
NORM_EPS = 1e-06
ROPE_BASE = 1000000.0
MASKED = -1e30


def gathered_once(array, axis):
    leaves = jax.tree.leaves(array)
    order = sorted(range(len(leaves)), key=lambda k: -leaves[k].size)
    width = (1, *leaves[order[0]].shape)[-1]
    lines = [
        jnp.pad(leaves[k].reshape(-1), (0, -leaves[k].size % width)).reshape(-1, width)
        for k in order
    ]
    both, at, found = (lax.all_gather(jnp.concatenate(lines), axis), 0, {})
    for k, line in zip(order, lines):
        slab = both[:, at : at + len(line)].reshape(len(both), -1)
        found[k] = slab[:, : leaves[k].size].reshape(-1, *leaves[k].shape)
        at += len(line)
    numbers = iter(range(len(leaves)))
    return jax.tree.map(lambda _: found[next(numbers)], array)


def combined_by_axis(array, axes, combine):
    for axis in axes:
        pieces = gathered_once(array, axis)
        array = jax.tree.map(lambda part: part[0], pieces)
        for k in range(1, lax.axis_size(axis)):
            array = combine(array, jax.tree.map(lambda part: part[k], pieces))
    return array


def sum_in_order(parts, axes, order):
    dims = [lax.axis_size(a) for a in axes]
    parts = parts.reshape(*dims, *parts.shape[1:])
    parts = parts.transpose(*order, *range(len(axes), parts.ndim))
    parts = parts.reshape(-1, *parts.shape[len(axes) :])
    for k in order:
        parts = lax.psum_scatter(parts, axes[k], scatter_dimension=0, tiled=True)
    return parts[0]


def cut_along(array, dim, devices):
    before, after = (array.shape[:dim], array.shape[dim + 1 :])
    return jnp.moveaxis(array.reshape(*before, devices, -1, *after), dim, 0)


def scatter_axes(array, axes, order, dim):
    devices = lax.axis_size(axes)
    return sum_in_order(cut_along(array, dim, devices), axes, order)


def rms_normalize(rows, gain):
    mean_square = jnp.mean(rows * rows, axis=-1, keepdims=True)
    return (rows * lax.rsqrt(mean_square + NORM_EPS) * gain.astype(jnp.float32)).astype(
        jnp.bfloat16
    )


def rotate(vectors, positions):
    half_dim = vectors.shape[-1] // 2
    frequency = ROPE_BASE ** (-2.0 * jnp.arange(half_dim, dtype=jnp.float32) / vectors.shape[-1])
    angles = positions.astype(jnp.float32)[..., None, None] * frequency
    cosine = jnp.cos(angles)
    sine_part = jnp.sin(angles)
    widened = vectors.astype(jnp.float32)
    first_half = widened[..., :half_dim]
    second = widened[..., half_dim:]
    joined = jnp.concatenate(
        [first_half * cosine - second * sine_part, second * cosine + first_half * sine_part],
        axis=-1,
    )
    return joined.astype(jnp.bfloat16)


def combine_partials(earlier, latter):
    top_one, total_one, sum_one = earlier
    top_two, total_two, sum_two = latter
    joined_top = jnp.maximum(top_one, top_two)
    scale_one = jnp.exp(top_one - joined_top)
    scale_two = jnp.exp(top_two - joined_top)
    return (
        joined_top,
        total_one * scale_one + total_two * scale_two,
        sum_one * scale_one[..., None] + sum_two * scale_two[..., None],
    )


def body(
    token_ids,
    lengths,
    embed_table,
    attn_gain,
    w_qkv,
    qkv_bias,
    cache_keys,
    cache_values,
    w_out,
    mlp_gain,
    w_gate,
    w_up,
    w_down,
):
    rank = lax.axis_index(SEQ)
    step_count, batch_count = token_ids.shape
    model_width = embed_table.shape[1]
    vocab_rows = embed_table.shape[0]
    query_width = HEADS * HEAD_DIM
    key_width = KV_HEADS * HEAD_DIM
    group_size = HEADS // KV_HEADS
    local_ids = token_ids - rank * vocab_rows
    inside = (local_ids >= 0) & (local_ids < vocab_rows)
    picked = jnp.take(embed_table, jnp.clip(local_ids, 0, vocab_rows - 1), axis=0)
    partial_rows = jnp.where(inside[..., None], picked.astype(jnp.float32), 0.0)
    stream = lax.psum(partial_rows, SEQ)
    normed = rms_normalize(stream, attn_gain).reshape(-1, model_width)
    feature_rows = w_qkv.shape[0]
    normed_local = lax.dynamic_slice_in_dim(normed, rank * feature_rows, feature_rows, 1)
    joint_partial = jnp.dot(normed_local, w_qkv, preferred_element_type=jnp.float32)
    joint_summed = lax.psum(joint_partial, SEQ)
    joint = (joint_summed + qkv_bias).astype(jnp.bfloat16).reshape(step_count, batch_count, -1)
    query_part = joint[..., :query_width].reshape(step_count, batch_count, HEADS, HEAD_DIM)
    key_part = joint[..., query_width : query_width + key_width].reshape(
        step_count, batch_count, KV_HEADS, HEAD_DIM
    )
    value_part = joint[..., query_width + key_width :].reshape(
        step_count, batch_count, KV_HEADS, HEAD_DIM
    )
    positions = lengths[None, :] + jnp.arange(step_count, dtype=jnp.int32)[:, None]
    queries = rotate(query_part, positions)
    new_keys = rotate(key_part, positions)
    grouped = queries.reshape(step_count, batch_count, KV_HEADS, group_size, HEAD_DIM)
    score_scale = 1.0 / math.sqrt(HEAD_DIM)
    local_len = cache_keys.shape[1]
    key_blocks = cache_keys.reshape(batch_count, local_len, KV_HEADS, HEAD_DIM)
    value_blocks = cache_values.reshape(batch_count, local_len, KV_HEADS, HEAD_DIM)
    scores = (
        jnp.einsum("sbkgd,bpkd->bkgsp", grouped, key_blocks, preferred_element_type=jnp.float32)
        * score_scale
    )
    places = rank * local_len + jnp.arange(local_len, dtype=jnp.int32)
    valid = (places[None, :] < lengths[:, None])[:, None, None, None, :]
    masked = jnp.where(valid, scores, MASKED)
    local_top = jnp.max(masked, axis=-1)
    weights = jnp.where(valid, jnp.exp(masked - local_top[..., None]), 0.0)
    local_total = jnp.sum(weights, axis=-1)
    local_sum = jnp.einsum(
        "bkgsp,bpkd->bkgsd",
        weights.astype(jnp.bfloat16),
        value_blocks,
        preferred_element_type=jnp.float32,
    )
    merged_top, merged_total, merged_sum = combined_by_axis(
        (local_top, local_total, local_sum), SEQ, combine_partials
    )
    new_scores = (
        jnp.einsum("sbkgd,tbkd->bkgst", grouped, new_keys, preferred_element_type=jnp.float32)
        * score_scale
    )
    step_index = jnp.arange(step_count, dtype=jnp.int32)
    causal = step_index[:, None] >= step_index[None, :]
    new_masked = jnp.where(causal, new_scores, MASKED)
    final_top = jnp.maximum(merged_top, jnp.max(new_masked, axis=-1))
    rescale = jnp.exp(merged_top - final_top)
    new_weights = jnp.where(causal, jnp.exp(new_masked - final_top[..., None]), 0.0)
    final_total = merged_total * rescale + jnp.sum(new_weights, axis=-1)
    final_sum = merged_sum * rescale[..., None] + jnp.einsum(
        "bkgst,tbkd->bkgsd",
        new_weights.astype(jnp.bfloat16),
        value_part,
        preferred_element_type=jnp.float32,
    )
    attended = jnp.transpose(final_sum / final_total[..., None], (3, 0, 1, 2, 4))
    attended = attended.reshape(step_count, batch_count, query_width).astype(jnp.bfloat16)
    shard_cols = w_out.shape[1]
    projected = jnp.dot(
        attended.reshape(-1, query_width), w_out, preferred_element_type=jnp.float32
    )
    stream_shard = lax.dynamic_slice_in_dim(stream, rank * shard_cols, shard_cols, 2)
    mid_shard = stream_shard + projected.reshape(step_count, batch_count, shard_cols)
    mid_rows = lax.all_gather(mid_shard, SEQ, axis=2, tiled=True)
    normed_mid = rms_normalize(mid_rows, mlp_gain)
    flat_rows = normed_mid.reshape(-1, model_width)
    gate = jnp.dot(flat_rows, w_gate, preferred_element_type=jnp.float32)
    upper = jnp.dot(flat_rows, w_up, preferred_element_type=jnp.float32)
    hidden = (jax.nn.silu(gate) * upper).astype(jnp.bfloat16)
    down_terms = jnp.dot(hidden, w_down, preferred_element_type=jnp.float32).reshape(
        step_count, batch_count, model_width
    )
    summed = scatter_axes(down_terms, SEQ, (2, 1, 0), 2)
    layer_out = (mid_shard + summed).astype(jnp.bfloat16)
    return (attended, layer_out)


def solution(mesh):
    finer = Mesh(
        mesh.devices.reshape(mesh.shape["parts"], 8, 8, 2), ("parts", "seq_0", "seq_1", "seq_2")
    )
    return jax.shard_map(
        body,
        mesh=finer,
        in_specs=(
            P(None, "parts"),
            P("parts"),
            P(SEQ, None),
            P(),
            P(SEQ, None),
            P(),
            P("parts", SEQ, None),
            P("parts", SEQ, None),
            P(None, SEQ),
            P(),
            P(None, SEQ),
            P(None, SEQ),
            P(SEQ, None),
        ),
        out_specs=(P(None, "parts", None), P(None, "parts", SEQ)),
        check_vma=False,
    )
```

profile of v0, /device:TPU:528, one launch (start us, length us, event | category | flops | bytes accessed | tf_op | source)
XLA Modules:
  0.0 717.2 jit_solution(17745230185070453889)
XLA Ops:
  7.3 0.8 compare_and_fusion
  8.3 4.2 gather_fusion
  12.8 0.8 convert_select_fusion
  14.0 0.3 copy.256
  14.4 1.1 copy-done.3
  15.5 0.3 copy.257
  15.8 1.1 bitcast_bitcast_fusion
  16.9 195.6 %all-reduce.14.cloned.1.call-done = f32[4,2,5120]{2,1,0:T(2,128)} async-done(((f32[4,2,5120]{2,1,0:T(2,128)}), f32[4,2,5120]{2,1,0:T(2,128)}) %all-reduce.14.cloned.1.call-update) | async-done | bytes 163856 | tf_op jit(solution)/shard_map/psum | solution.py:125
  212.4 1.1 multiply_reduce_fusion.1
  213.5 1.1 multiply_convert_fusion.1
  214.6 1.0 fusion.77
  215.8 181.4 %all-reduce.16.cloned.1.call-done = f32[8,7168]{1,0:T(8,128)} async-done(((f32[8,7168]{1,0:T(8,128)}), f32[8,7168]{1,0:T(8,128)}) %all-reduce.16.cloned.1.call-update) | async-done | bytes 229392 | tf_op jit(solution)/shard_map/psum | solution.py:130
  397.2 1.0 add_convert_fusion
  398.3 0.3 subtract_convert_fusion
  398.6 0.5 fusion.92
  399.2 0.2 copy.205
  399.4 0.3 fusion.13
  400.1 1.5 fusion.9
  401.6 0.7 maximum_bitcast_fusion
  402.4 38.6 %all-gather.9.cloned.1.call-done = f32[8,326,128]{2,1,0:T(8,128)} async-done(((f32[1,326,128]{2,1,0:T(8,128)}), f32[8,326,128]{2,1,0:T(8,128)}) %all-gather.9.cloned.1.call-update) | async-done | bytes 1335312 | tf_op jit(solution)/shard_map/all_gather | solution.py:25
  441.0 0.8 fusion.88
  442.1 2.0 fusion.39
  444.1 0.7 maximum_bitcast_fusion.1
  445.1 0.8 fusion.93
  446.0 38.5 %all-gather.11.cloned.1.call-done = f32[8,326,128]{2,1,0:T(8,128)} async-done(((f32[1,326,128]{2,1,0:T(8,128)}), f32[8,326,128]{2,1,0:T(8,128)}) %all-gather.11.cloned.1.call-update) | async-done | bytes 1335312 | tf_op jit(solution)/shard_map/all_gather | solution.py:25
  484.5 0.8 fusion.87
  485.6 2.0 fusion.18
  487.6 2.1 all-gather.5
  491.8 0.5 fusion.4
  492.4 0.4 copy-done.10
  492.8 1.0 convolution_add_fusion.1
  493.9 56.9 %all_gather.27 = f32[4,2,5120]{0,1,2:T(2,128)} all-gather(f32[4,2,40]{0,1,2:T(2,128)S(1)} %copy.230), channel_id=1, replica_groups=mesh['parts'=2,'seq_0'=8,'seq_1'=8,'seq_2'=2] {'seq_0','seq_1','seq_2'}, dimensions={2}, use_global_device_ids=true | all-gather | bytes 165120 | tf_op jit(solution)/shard_map/all_gather | solution.py:191
  550.8 5.6 copy.233
  556.5 7.0 multiply_reduce_fusion
  564.0 0.3 fusion.94
  564.2 1.9 fusion.8
  566.1 0.4 reshape_reshape.2
  566.7 1.1 copy.236
  568.0 0.6 dynamic-slice
  569.3 30.1 %all-reduce.18.cloned.1.call-done = f32[128,4,2,40]{3,1,2,0:T(4,128)} async-done(((f32[128,4,2,40]{3,1,2,0:T(4,128)}), f32[128,4,2,40]{3,1,2,0:T(4,128)}) %all-reduce.18.cloned.1.call-update) | async-done | bytes 163856
  599.4 1.7 constant_dynamic-slice_fusion.2
  601.1 0.6 dynamic-slice.2
  601.7 0.6 dynamic-slice.4
  603.0 75.6 %all-reduce.20.cloned.1.call-done = f32[64,4,2,40]{3,1,2,0:T(4,128)} async-done(((f32[64,4,2,40]{3,1,2,0:T(4,128)}), f32[64,4,2,40]{3,1,2,0:T(4,128)}) %all-reduce.20.cloned.1.call-update) | async-done | bytes 81936
  678.7 0.8 constant_dynamic-slice_fusion.1
  679.4 29.7 %all-reduce.8 = f32[8,4,2,40]{3,1,2,0:T(4,128)S(1)} all-reduce(f32[8,4,2,40]{3,1,2,0:T(4,128)S(1)} %constant_dynamic-slice_fusion.1), channel_id=7, replica_groups=mesh['parts'=2,'seq_0'=8,'seq_1'=8,'seq_2'=2] {'seq_0'}, use_global_device_ids=true, to_apply=%region_10.11.clone | all-reduce | flops 2560 | bytes 20480
  709.1 0.6 constant_dynamic-slice_fusion
  709.7 0.6 fusion.70
  (121 shorter events, 5.7 us)
Async XLA Ops:
  7.2 557.1 %copy-start = (bf16[128,5120]{1,0:T(8,128)(2,1)S(1)}, bf16[128,5120]{1,0:T(8,128)(2,1)}, u32[]{:S(2)}) copy-start(bf16[128,5120]{1,0:T(8,128)(2,1)} %param.25) | copy-start | bytes 3932164
  7.2 6.6 copy-start.7
  7.2 6.6 copy-start.9
  7.2 6.8 copy-start.2
  7.2 205.2 %all-reduce.14.cloned.1.call-start = ((), (), s32[]{:S(2)}) async-start(), calls=%async_computation | async-start | bytes 327680 | tf_op jit(solution)/shard_map/psum | solution.py:125
  13.7 383.5 %all-reduce.16.cloned.1.call-start = ((), (), s32[]{:S(2)}) async-start(), calls=%async_computation.1 | async-start | bytes 458752 | tf_op jit(solution)/shard_map/psum | solution.py:130
  14.3 1.2 copy-start.3
  15.8 198.8 %copy-start.4 = (bf16[40,7168]{1,0:T(8,128)(2,1)S(1)}, bf16[40,7168]{1,0:T(8,128)(2,1)}, u32[]{:S(2)}) copy-start(bf16[40,7168]{1,0:T(8,128)(2,1)} %param.17) | copy-start | bytes 1720324
  16.9 380.3 %copy-start.6 = (f32[7168]{0:T(1024)S(1)}, f32[7168]{0:T(1024)}, u32[]{:S(2)}) copy-start(f32[7168]{0:T(1024)} %param.18) | copy-start | bytes 86020
  215.7 225.3 %all-gather.9.cloned.1.call-start = ((), (), s32[]{:S(2)}) async-start(), calls=%async_computation.2 | async-start | bytes 1511424 | tf_op jit(solution)/shard_map/all_gather | solution.py:25
  402.3 42.6 %copy-start.8 = (bf16[5120]{0:T(1024)(128)(2,1)S(1)}, bf16[5120]{0:T(1024)(128)(2,1)}, u32[]{:S(2)}) copy-start(bf16[5120]{0:T(1024)(128)(2,1)} %param.22) | copy-start | bytes 30724
  402.3 82.2 %all-gather.11.cloned.1.call-start = ((), (), s32[]{:S(2)}) async-start(), calls=%async_computation.3 | async-start | bytes 1511424 | tf_op jit(solution)/shard_map/all_gather | solution.py:25
  444.8 154.6 %all-reduce.18.cloned.1.call-start = ((), (), s32[]{:S(2)}) async-start(), calls=%async_computation.4 | async-start | bytes 1048576
  491.8 1.0 copy-start.10
  492.8 58.0 %copy-start.5 = (bf16[4,2,5120]{2,1,0:T(2,128)(2,1)}, bf16[4,2,5120]{2,1,0:T(2,128)(2,1)S(1)}, u32[]{:S(2)}) copy-start(bf16[4,2,5120]{2,1,0:T(2,128)(2,1)S(1)} %convert_element_type.84) | copy-start | bytes 245764
  556.5 7.5 %copy-start.1 = (bf16[5120,128]{1,0:T(8,128)(2,1)S(1)}, bf16[5120,128]{1,0:T(8,128)(2,1)}, u32[]{:S(2)}) copy-start(bf16[5120,128]{1,0:T(8,128)(2,1)} %param.23) | copy-start | bytes 3932164
  566.5 1.5 copy-start.13
  566.7 34.4 %copy-start.12 = (u32[256]{0:T(256)S(1)}, u32[256]{0:T(256)}, u32[]{:S(2)}) copy-start(u32[256]{0:T(256)} %constant.90) | copy-start | bytes 3076
  566.7 35.0 %copy-start.11 = (u32[256]{0:T(256)S(1)}, u32[256]{0:T(256)}, u32[]{:S(2)}) copy-start(u32[256]{0:T(256)} %constant.94) | copy-start | bytes 3076
  567.9 110.7 %all-reduce.20.cloned.1.call-start = ((), (), s32[]{:S(2)}) async-start(), calls=%async_computation.5 | async-start | bytes 524288
Sparse Core Ops, SparseCore 0:
  13.8 198.6 all-reduce.13
  215.8 181.3 all-reduce.15
  402.5 38.5 all-gather.8
  444.9 39.5 all-gather.10
  568.1 31.3 all-reduce.17
  601.6 77.0 all-reduce.19
where the time goes:
time: 718 us; the launch traced here: 717 us
  waiting for transfers between devices  560 us (78%)
  blocking collectives  88.7 us (12%)
  local copies, waits for them, and re-layouts  25.4 us (4%)
  other arithmetic  19.2 us (3%)
  between operations  16 us (2%)
  matrix products  7.37 us (1%)
    psum x1, waiting for transfers between devices, body(): stream = lax.psum(partial_rows, SEQ)  196 us
    psum x1, waiting for transfers between devices, body(): joint_summed = lax.psum(joint_partial, SEQ)  181 us
    unnamed x8, waiting for transfers between devices  106 us
    all_gather x2, waiting for transfers between devices, gathered_once(): both, at, found = (lax.all_gather(jnp.concatenate(lines), axis), 0, {})  77.1 us
    all_gather x1, blocking collectives, body(): mid_rows = lax.all_gather(mid_shard, SEQ, axis=2, tiled=True)  56.9 us
    unnamed x1, blocking collectives  29.7 us
  transfers between devices with their start and end apart: 6, of which 6 were waited for; matrix products, arithmetic and copies ran while one was open for 1% of the time, Pallas kernels for 0%

commit v1 on v0

--- a/solution.py
+++ b/solution.py
@@ -127,7 +127,7 @@
     feature_rows = w_qkv.shape[0]
     normed_local = lax.dynamic_slice_in_dim(normed, rank * feature_rows, feature_rows, 1)
     joint_partial = jnp.dot(normed_local, w_qkv, preferred_element_type=jnp.float32)
-    joint_summed = lax.psum(joint_partial, SEQ)
+    joint_summed = jnp.sum(lax.all_gather(joint_partial, SEQ), axis=0)
     joint = (joint_summed + qkv_bias).astype(jnp.bfloat16).reshape(step_count, batch_count, -1)
     query_part = joint[..., :query_width].reshape(step_count, batch_count, HEADS, HEAD_DIM)
     key_part = joint[..., query_width : query_width + key_width].reshape(

time: 718 us -> 671 us (0.935)
  waiting for transfers between devices: 560 us -> 504 us
  other arithmetic: 19.2 us -> 28.9 us
    psum x1 -> x0, waiting for transfers between devices: 181 us -> none  [body(): joint_summed = lax.psum(joint_partial, SEQ)]
    all_gather x0 -> x1, waiting for transfers between devices: none -> 121 us  [body(): joint_summed = jnp.sum(lax.all_gather(joint_partial, SEQ), axis=0)]
    reduce_sum x0 -> x1, other arithmetic: none -> 10.6 us  [body(): joint_summed = jnp.sum(lax.all_gather(joint_partial, SEQ), axis=0)]
where the time goes in v1:
time: 671 us; the launch traced here: 670 us
  waiting for transfers between devices  504 us (75%)
  blocking collectives  88.7 us (13%)
  other arithmetic  28.9 us (4%)
  local copies, waits for them, and re-layouts  25 us (4%)
  between operations  16 us (2%)
  matrix products  7.37 us (1%)
    psum x1, waiting for transfers between devices, body(): stream = lax.psum(partial_rows, SEQ)  199 us
    all_gather x1, waiting for transfers between devices, body(): joint_summed = jnp.sum(lax.all_gather(joint_partial, SEQ), axis=0)  121 us
    unnamed x8, waiting for transfers between devices  106 us
    all_gather x2, waiting for transfers between devices, gathered_once(): both, at, found = (lax.all_gather(jnp.concatenate(lines), axis), 0, {})  78 us
    all_gather x1, blocking collectives, body(): mid_rows = lax.all_gather(mid_shard, SEQ, axis=2, tiled=True)  56.9 us
    unnamed x1, blocking collectives  29.7 us
  transfers between devices with their start and end apart: 6, of which 6 were waited for; matrix products, arithmetic and copies ran while one was open for 1% of the time, Pallas kernels for 0%

profile of v1, /device:TPU:528, one launch (start us, length us, event | category | flops | bytes accessed | tf_op | source)
XLA Modules:
  0.0 669.9 jit_solution(16616535544786436360)
XLA Ops:
  7.3 0.8 compare_and_fusion
  8.3 4.3 gather_fusion
  12.9 0.8 convert_select_fusion
  13.8 198.7 %all-reduce.13.cloned.1.call-done = f32[4,2,5120]{2,1,0:T(2,128)} async-done(((f32[4,2,5120]{2,1,0:T(2,128)}), f32[4,2,5120]{2,1,0:T(2,128)}) %all-reduce.13.cloned.1.call-update) | async-done | bytes 163856 | tf_op jit(solution)/shard_map/psum | solution.py:125
  212.5 1.1 multiply_reduce_fusion.1
  213.6 1.1 multiply_convert_fusion.1
  214.7 1.0 fusion.77
  216.1 0.3 copy.256
  216.4 0.6 copy-done.3
  216.9 0.3 copy.257
  217.4 1.1 bitcast_bitcast_fusion
  218.5 120.8 %all-gather.11.cloned.1.call-done = f32[1024,7168]{1,0:T(8,128)} async-done(((f32[8,7168]{1,0:T(8,128)}), f32[1024,7168]{1,0:T(8,128)}) %all-gather.11.cloned.1.call-update) | async-done | bytes 29360144 | tf_op jit(solution)/shard_map/all_gather | solution.py:130
  339.2 10.6 %bitcast_reduce_fusion = f32[8,7168]{1,0:T(8,128)S(1)} fusion(f32[1024,7168]{1,0:T(8,128)} %all-gather.11.cloned.1.call-done), kind=kLoop, calls=%fused_computation.1 | loop fusion | flops 7282688 | bytes 29589504 | tf_op jit(solution)/shard_map/reduce_sum | solution.py:130
  350.2 0.3 subtract_convert_fusion
  350.5 0.5 fusion.92
  351.2 0.3 fusion.13
  351.5 0.2 copy.206
  351.9 1.5 fusion.9
  353.5 0.7 maximum_bitcast_fusion
  354.3 39.5 %all-gather.13.cloned.1.call-done = f32[8,326,128]{2,1,0:T(8,128)} async-done(((f32[1,326,128]{2,1,0:T(8,128)}), f32[8,326,128]{2,1,0:T(8,128)}) %all-gather.13.cloned.1.call-update) | async-done | bytes 1335312 | tf_op jit(solution)/shard_map/all_gather | solution.py:25
  393.8 0.8 fusion.88
  394.8 2.0 fusion.39
  396.8 0.7 maximum_bitcast_fusion.1
  397.8 0.8 fusion.93
  398.8 38.5 %all-gather.15.cloned.1.call-done = f32[8,326,128]{2,1,0:T(8,128)} async-done(((f32[1,326,128]{2,1,0:T(8,128)}), f32[8,326,128]{2,1,0:T(8,128)}) %all-gather.15.cloned.1.call-update) | async-done | bytes 1335312 | tf_op jit(solution)/shard_map/all_gather | solution.py:25
  437.3 0.8 fusion.87
  438.3 2.0 fusion.18
  440.3 2.1 all-gather.6
  444.5 0.5 fusion.4
  445.1 0.4 copy-done.10
  445.5 1.0 convolution_add_fusion.1
  446.6 56.9 %all_gather.35 = f32[4,2,5120]{0,1,2:T(2,128)} all-gather(f32[4,2,40]{0,1,2:T(2,128)S(1)} %copy.230), channel_id=1, replica_groups=mesh['parts'=2,'seq_0'=8,'seq_1'=8,'seq_2'=2] {'seq_0','seq_1','seq_2'}, dimensions={2}, use_global_device_ids=true | all-gather | bytes 165120 | tf_op jit(solution)/shard_map/all_gather | solution.py:191
  503.6 5.6 copy.233
  509.2 7.0 %multiply_reduce_fusion = f32[4,2]{0,1:T(2,128)S(1)} fusion(f32[4,2,5120]{0,1,2:T(2,128)} %all_gather.35), kind=kLoop, calls=%fused_computation.2 | loop fusion | flops 81912 | bytes 163872 | tf_op jit(solution)/shard_map/reduce_sum | solution.py:64
  516.7 0.3 fusion.94
  517.0 1.9 fusion.8
  518.9 0.4 reshape_reshape.2
  519.5 1.1 copy.236
  520.8 0.6 dynamic-slice
  522.0 30.1 %all-reduce.15.cloned.1.call-done = f32[128,4,2,40]{3,1,2,0:T(4,128)} async-done(((f32[128,4,2,40]{3,1,2,0:T(4,128)}), f32[128,4,2,40]{3,1,2,0:T(4,128)}) %all-reduce.15.cloned.1.call-update) | async-done | bytes 163856
  552.2 1.7 constant_dynamic-slice_fusion.2
  553.9 0.6 dynamic-slice.2
  554.5 0.6 dynamic-slice.4
  555.8 75.6 %all-reduce.17.cloned.1.call-done = f32[64,4,2,40]{3,1,2,0:T(4,128)} async-done(((f32[64,4,2,40]{3,1,2,0:T(4,128)}), f32[64,4,2,40]{3,1,2,0:T(4,128)}) %all-reduce.17.cloned.1.call-update) | async-done | bytes 81936
  631.4 0.8 constant_dynamic-slice_fusion.1
  632.2 29.7 %all-reduce.8 = f32[8,4,2,40]{3,1,2,0:T(4,128)S(1)} all-reduce(f32[8,4,2,40]{3,1,2,0:T(4,128)S(1)} %constant_dynamic-slice_fusion.1), channel_id=8, replica_groups=mesh['parts'=2,'seq_0'=8,'seq_1'=8,'seq_2'=2] {'seq_0'}, use_global_device_ids=true, to_apply=%region_10.11.clone | all-reduce | flops 2560 | bytes 20480
  661.9 0.6 constant_dynamic-slice_fusion
  662.5 0.6 fusion.70
  (122 shorter events, 5.9 us)
Async XLA Ops:
  7.2 509.8 %copy-start = (bf16[128,5120]{1,0:T(8,128)(2,1)S(1)}, bf16[128,5120]{1,0:T(8,128)(2,1)}, u32[]{:S(2)}) copy-start(bf16[128,5120]{1,0:T(8,128)(2,1)} %param.25) | copy-start | bytes 3932164
  7.2 6.6 copy-start.7
  7.2 207.5 %copy-start.4 = (bf16[40,7168]{1,0:T(8,128)(2,1)S(1)}, bf16[40,7168]{1,0:T(8,128)(2,1)}, u32[]{:S(2)}) copy-start(bf16[40,7168]{1,0:T(8,128)(2,1)} %param.17) | copy-start | bytes 1720324
  7.2 205.3 %all-reduce.13.cloned.1.call-start = ((), (), s32[]{:S(2)}) async-start(), calls=%async_computation | async-start | bytes 327680 | tf_op jit(solution)/shard_map/psum | solution.py:125
  8.3 207.6 %copy-start.9 = (s32[2]{0:T(128)S(1)}, s32[2]{0:T(128)}, u32[]{:S(2)}) copy-start(s32[2]{0:T(128)} %param.14) | copy-start | bytes 28
  8.3 207.8 %copy-start.2 = (bf16[2,256,1024]{2,1,0:T(8,128)(2,1)S(1)}, bf16[2,256,1024]{2,1,0:T(8,128)(2,1)}, u32[]{:S(2)}) copy-start(bf16[2,256,1024]{2,1,0:T(8,128)(2,1)} %param.19) | copy-start | bytes 3145732
  13.7 325.5 %all-gather.11.cloned.1.call-start = ((), (), s32[]{:S(2)}) async-start(), calls=%async_computation.1 | async-start | bytes 29589504 | tf_op jit(solution)/shard_map/all_gather | solution.py:130
  215.7 1.2 copy-start.3
  215.8 178.0 %all-gather.13.cloned.1.call-start = ((), (), s32[]{:S(2)}) async-start(), calls=%async_computation.2 | async-start | bytes 1511424 | tf_op jit(solution)/shard_map/all_gather | solution.py:25
  218.5 131.5 %copy-start.6 = (f32[7168]{0:T(1024)S(1)}, f32[7168]{0:T(1024)}, u32[]{:S(2)}) copy-start(f32[7168]{0:T(1024)} %param.18) | copy-start | bytes 86020
  354.1 43.5 %copy-start.8 = (bf16[5120]{0:T(1024)(128)(2,1)S(1)}, bf16[5120]{0:T(1024)(128)(2,1)}, u32[]{:S(2)}) copy-start(bf16[5120]{0:T(1024)(128)(2,1)} %param.22) | copy-start | bytes 30724
  354.2 83.1 %all-gather.15.cloned.1.call-start = ((), (), s32[]{:S(2)}) async-start(), calls=%async_computation.3 | async-start | bytes 1511424 | tf_op jit(solution)/shard_map/all_gather | solution.py:25
  397.5 154.6 %all-reduce.15.cloned.1.call-start = ((), (), s32[]{:S(2)}) async-start(), calls=%async_computation.4 | async-start | bytes 1048576
  444.5 1.0 copy-start.10
  445.5 58.0 %copy-start.5 = (bf16[4,2,5120]{2,1,0:T(2,128)(2,1)}, bf16[4,2,5120]{2,1,0:T(2,128)(2,1)S(1)}, u32[]{:S(2)}) copy-start(bf16[4,2,5120]{2,1,0:T(2,128)(2,1)S(1)} %convert_element_type.85) | copy-start | bytes 245764
  509.2 7.5 %copy-start.1 = (bf16[5120,128]{1,0:T(8,128)(2,1)S(1)}, bf16[5120,128]{1,0:T(8,128)(2,1)}, u32[]{:S(2)}) copy-start(bf16[5120,128]{1,0:T(8,128)(2,1)} %param.23) | copy-start | bytes 3932164
  519.3 1.5 copy-start.13
  519.5 34.4 %copy-start.12 = (u32[256]{0:T(256)S(1)}, u32[256]{0:T(256)}, u32[]{:S(2)}) copy-start(u32[256]{0:T(256)} %constant.90) | copy-start | bytes 3076
  519.5 35.0 %copy-start.11 = (u32[256]{0:T(256)S(1)}, u32[256]{0:T(256)}, u32[]{:S(2)}) copy-start(u32[256]{0:T(256)} %constant.94) | copy-start | bytes 3076
  520.7 110.7 %all-reduce.17.cloned.1.call-start = ((), (), s32[]{:S(2)}) async-start(), calls=%async_computation.5 | async-start | bytes 524288
Sparse Core Ops, SparseCore 0:
  13.8 198.6 all-reduce.12
  215.9 123.3 all-gather.10
  354.3 39.3 all-gather.12
  397.7 39.5 all-gather.14
  520.8 31.3 all-reduce.14
  554.4 77.0 all-reduce.16
